TPU v7x, 32 devices: a whole 2x2x4 slice. The times are simulated.
32 devices in a mesh: ep: 8 (over y, x, core), dp: 4 (over z).
Axes of the slice: x: 2, y: 2, z: 4, core: 2. Of those that a mesh axis runs over, the one named last changes fastest.
Arguments:
- master_weights: float32 [8, 1024, 3584], P('ep', 'dp'), may hold values from -6 to 6
- first_moment: float32 [8, 1024, 3584], P('ep', 'dp'), may hold values from -6 to 6
- second_moment: float32 [8, 1024, 3584], P('ep', 'dp'), may hold values from 0.01 to 4
- expert_ids: int32 [8], replicated, may hold values from 0 to 255, as said below
- bucket_offsets: int32 [1024], replicated, may hold values from 0 to 1023, as said below
- writer_rank: int32 [1024], replicated, may hold values from 0 to 3, as said below
Outputs:
- saved: bfloat16 [3, 8, 1024, 3584], P(None, 'ep', 'dp')
Inputs may be any that keep to these rules, and one draw needn't show every extreme that they name: `expert_ids`: 8 different global expert numbers. `bucket_offsets`: each saved row named exactly once. `writer_rank`: of the bucket rows held by any one dp index, exactly 1024 // (4 * 4) are written by each dp index.
All inputs are finite; a program needn't handle non-finite values.
Results may differ from a plain program's by a relative error of at most 0.001.
Values may be sent and summed in bfloat16 or wider, within the bound.
A program may use at most 128 MiB of HBM per device.

v0:
```python
import functools
import math

import jax
import jax.numpy as jnp
from jax import lax
from jax.experimental import pallas as pl
from jax.experimental.pallas import tpu as pltpu
from jax.sharding import PartitionSpec as P

MESH = pl.DeviceIdType.MESH
FIELDS = 3


def tables(bucket_offsets, writer_rank, mine, groups):
    total = bucket_offsets.shape[0]
    shard = total // groups
    pair = shard // groups
    p = jnp.arange(total, dtype=jnp.int32)
    q = jnp.arange(shard, dtype=jnp.int32)
    earlier = (writer_rank[None, :] == writer_rank[:, None]) & (p[None, :] < p[:, None])
    place = writer_rank * shard + jnp.sum(earlier.astype(jnp.int32), axis=1)
    target = jnp.sum(jnp.where(bucket_offsets[:, None] == p[None, :], place[None, :], 0), axis=1)
    dest = (target // shard).reshape(groups, shard)
    ahead = (dest[:, None, :] == dest[:, :, None]) & (q[None, None, :] < q[None, :, None])
    rank = jnp.sum(ahead.astype(jnp.int32), axis=2)
    position = lax.dynamic_index_in_dim(dest * pair + rank, mine, 0)
    arrives = jnp.arange(groups, dtype=jnp.int32)[:, None] * pair + rank
    return position, target.reshape(1, total), arrives.reshape(1, total)


def order_of(expert_ids):
    count = expert_ids.shape[0]
    k = jnp.arange(count, dtype=jnp.int32)
    rank = jnp.sum((expert_ids[None, :] < expert_ids[:, None]).astype(jnp.int32), axis=1)
    return jnp.sum(jnp.where(rank[None, :] == k[:, None], k[None, :], 0), axis=1)


def one_hot(index_ref, first, depth):
    rows = lax.broadcasted_iota(jnp.int32, (depth, index_ref.shape[1]), 0) + first
    return (index_ref[...] == rows).astype(jnp.float32).astype(jnp.bfloat16)


def rounded_dot(left, right):
    return jnp.dot(left, right, preferred_element_type=jnp.float32).astype(jnp.bfloat16)


def column_tiles(cols, body):
    tile = cols // 2 if cols % 256 == 0 else cols

    @pl.loop(0, cols // tile)
    def _(i):
        body(pl.ds(pl.multiple_of(i * tile, tile), tile))


def partner(me, offset, n):
    out, bit = 0, 1
    while bit < n:
        out = out + ((me // bit + (offset // bit) % 2) % 2) * bit
        bit *= 2
    return out


def exchange_kernel(n_ep, n_dp, half, *refs_in):
    order_ref, position_ref, target_ref, arrives_ref = refs_in[:4]
    fields_in, out_ref, scratch = refs_in[4 : 4 + FIELDS], refs_in[4 + FIELDS], refs_in[5 + FIELDS :]
    e1 = scratch[: 2 * FIELDS]
    wide, ready, sel, mid, placed, late, before, after = scratch[2 * FIELDS : 2 * FIELDS + 8]
    load, z_send, z_recv, a_send, a_recv, b_send, b_recv, store = scratch[2 * FIELDS + 8 :]
    ep, dp = lax.axis_index("ep"), lax.axis_index("dp")
    _, blocks, depth, cols = out_ref.shape
    rows = blocks * depth
    aligned = depth % 16 == 0
    m_ep, m_dp = blocks // n_ep, blocks // n_dp
    z_order = sorted(range(1, n_dp), key=lambda o: -o)
    e_order = sorted(range(1, n_ep), key=lambda o: (o == 1, o % 2, -o))
    first = pl.ds(0, half)
    last = pl.ds(half, cols - half)

    def span(c):
        return first if c < FIELDS else last

    def load_copy(c):
        return pltpu.make_async_copy(fields_in[c % FIELDS].at[:, span(c)], wide.at[c], load.at[c])

    turns = [c for f in range(FIELDS) for c in (f, FIELDS + f)]
    for c in turns:
        load_copy(c).start()

    barrier = pltpu.get_barrier_semaphore()
    for o in range(1, n_dp):
        pl.semaphore_signal(barrier, inc=1, device_id={"dp": partner(dp, o, n_dp)}, device_id_type=MESH)
    for o in range(1, n_ep):
        pl.semaphore_signal(barrier, inc=1, device_id={"ep": partner(ep, o, n_ep)}, device_id_type=MESH)

    def remote(src, dst, send, recv, axis, peer):
        return pltpu.make_async_remote_copy(
            src_ref=src, dst_ref=dst, send_sem=send, recv_sem=recv,
            device_id={axis: peer}, device_id_type=MESH,
        )

    def z_refs(c):
        return (ready.at[c], mid.at[c]) if c < FIELDS else (mid.at[c], late.at[c - FIELDS])

    def a_ref(c):
        return placed.at[c] if c < FIELDS else ready.at[c]

    def b_ref(c):
        return out_ref.at[c, :, :, first] if c < FIELDS else mid.at[c]

    def z_copies(c):
        src, dst = z_refs(c)
        return [
            remote(
                src.at[pl.ds(partner(dp, o, n_dp) * m_dp, m_dp)], dst.at[pl.ds(dp * m_dp, m_dp)],
                z_send.at[c, o], z_recv.at[c, o], "dp", partner(dp, o, n_dp),
            )
            for o in z_order
        ]

    def a_copies(c):
        return [
            remote(
                a_ref(c).at[pl.ds(partner(ep, o, n_ep) * m_ep, m_ep)], e1[c].at[ep],
                a_send.at[c, o], a_recv.at[c, o], "ep", partner(ep, o, n_ep),
            )
            for o in e_order
        ]

    def b_copies(c):
        return [
            remote(
                sel.at[c, partner(ep, o, n_ep)], b_ref(c).at[pl.ds(ep * m_ep, m_ep)],
                b_send.at[c, o], b_recv.at[c, o], "ep", partner(ep, o, n_ep),
            )
            for o in e_order
        ]

    def start(copies):
        for copy in copies:
            copy.start()

    def arrive(copies):
        for copy in copies:
            copy.wait_recv()

    def own_out(c):
        own = pl.ds(ep * m_ep, m_ep)
        return pltpu.make_async_copy(sel.at[c, ep], out_ref.at[c, own, :, first], store.at[c])

    def placed_out(c):
        return pltpu.make_async_copy(placed.at[c], out_ref.at[c - FIELDS, :, :, last], store.at[c])

    def sort(c):
        load_copy(c).wait()

        def body(part):
            x = wide[c, :, part].astype(jnp.bfloat16)
            if aligned:
                ready[c, :, :, part] = rounded_dot(before[...], x).reshape(blocks, depth, x.shape[1])
            else:
                @pl.loop(0, blocks)
                def _(i):
                    ready[c, i, :, part] = rounded_dot(one_hot(position_ref, i * depth, depth), x)

        column_tiles(half, body)

    def place(c, src):
        def body(part):
            if aligned:
                x = src[:, :, part].reshape(rows, part.size)
                placed[c, :, :, part] = rounded_dot(after[...], x).reshape(blocks, depth, part.size)
            else:
                @pl.loop(0, blocks)
                def _(i):
                    def add(j, total):
                        return total + jnp.dot(
                            after[i, j], src[j, :, part], preferred_element_type=jnp.float32
                        )

                    total = lax.fori_loop(0, blocks, add, jnp.zeros((depth, part.size), jnp.float32))
                    placed[c, i, :, part] = total.astype(jnp.bfloat16)

        column_tiles(half, body)

    def after_of(i, j, size):
        return lax.dot_general(
            one_hot(target_ref, dp * rows + i * size, size), one_hot(arrives_ref, j * size, size),
            (((1,), (1,)), ((), ())), preferred_element_type=jnp.float32,
        ).astype(jnp.bfloat16)

    def z_start(c):
        start(z_copies(c))
        src, dst = z_refs(c)
        own = pl.ds(dp * m_dp, m_dp)
        dst[own] = src[own]

    def a_start(c):
        start(a_copies(c))
        e1[c][ep] = a_ref(c)[pl.ds(ep * m_ep, m_ep)]

    def a_to_b(c):
        arrive(a_copies(c))
        for k in range(n_ep):
            sel[c, k] = e1[c][order_ref[k]]
        start(b_copies(c))
        if c < FIELDS:
            own_out(c).start()
        else:
            mid[c, pl.ds(ep * m_ep, m_ep)] = sel[c, ep]

    def z_to_a(c):
        arrive(z_copies(c))
        place(c, mid.at[c])
        a_start(c)

    def b_to_z(c):
        arrive(b_copies(c))
        z_start(c)

    def finish(c):
        arrive(z_copies(c))
        place(c, late.at[c - FIELDS])
        placed_out(c).start()

    if aligned:
        before[...] = one_hot(position_ref, 0, rows)
    for c in turns:
        sort(c)
        if c == 0:
            pl.semaphore_wait(barrier, n_dp + n_ep - 2)
        (z_start if c < FIELDS else a_start)(c)
    if aligned:
        after[...] = after_of(0, 0, rows)
    else:
        @pl.loop(0, blocks)
        def _(i):
            @pl.loop(0, blocks)
            def _(j):
                after[i, j] = after_of(i, j, depth)
    a_to_b(3)
    a_to_b(4)
    z_to_a(0)
    a_to_b(5)
    b_to_z(3)
    z_to_a(1)
    b_to_z(4)
    a_to_b(0)
    z_to_a(2)
    b_to_z(5)
    finish(3)
    a_to_b(1)
    a_to_b(2)
    finish(4)
    for c in range(FIELDS):
        arrive(b_copies(c))
    finish(5)
    for c in range(2 * FIELDS):
        for copies in (z_copies(c), a_copies(c), b_copies(c)):
            for copy in copies:
                copy.wait_send()
        (own_out if c < FIELDS else placed_out)(c).wait()


def exchange(order, indices, arrays, n_ep, n_dp):
    rows, cols = arrays[0].shape
    depth = math.gcd(rows // n_dp, rows // n_ep)
    blocks = rows // depth
    half = cols // 2
    per = blocks // n_ep
    chunks = 2 * FIELDS
    bf16, dma = jnp.bfloat16, pltpu.SemaphoreType.DMA
    vmem = pl.BlockSpec(memory_space=pltpu.VMEM)
    anywhere = pl.BlockSpec(memory_space=pl.ANY)
    square = (rows, rows) if depth % 16 == 0 else (blocks, blocks, depth, depth)
    return pl.pallas_call(
        functools.partial(exchange_kernel, n_ep, n_dp, half),
        out_shape=jax.ShapeDtypeStruct((FIELDS, blocks, depth, cols), bf16),
        in_specs=[pl.BlockSpec(memory_space=pltpu.SMEM), vmem, vmem, vmem] + [anywhere] * FIELDS,
        out_specs=anywhere,
        scratch_shapes=[pltpu.VMEM((n_ep, per, depth, half), bf16)] * chunks
        + [
            pltpu.VMEM((chunks, rows, half), jnp.float32),
            pltpu.VMEM((chunks, blocks, depth, half), bf16),
            pltpu.VMEM((chunks, n_ep, per, depth, half), bf16),
            pltpu.VMEM((chunks, blocks, depth, half), bf16),
            pltpu.VMEM((chunks, blocks, depth, half), bf16),
            pltpu.VMEM((FIELDS, blocks, depth, half), bf16),
            pltpu.VMEM(square, bf16),
            pltpu.VMEM(square, bf16),
            dma((chunks,)),
            dma((chunks, n_dp)),
            dma((chunks, n_dp)),
            dma((chunks, n_ep)),
            dma((chunks, n_ep)),
            dma((chunks, n_ep)),
            dma((chunks, n_ep)),
            dma((chunks,)),
        ],
        compiler_params=pltpu.CompilerParams(collective_id=0, has_side_effects=True),
    )(order, *indices, *arrays)


def on_device(master_weights, first_moment, second_moment, expert_ids, bucket_offsets, writer_rank):
    n_dp, n_ep = lax.axis_size("dp"), lax.axis_size("ep")
    _, rows, cols = master_weights.shape
    indices = tables(bucket_offsets, writer_rank, lax.axis_index("dp"), n_dp)
    arrays = (master_weights[0], first_moment[0], second_moment[0])
    saved = exchange(order_of(expert_ids), indices, arrays, n_ep, n_dp)
    return saved.reshape(FIELDS, 1, rows, cols)


def solution(mesh):
    return jax.shard_map(
        on_device,
        mesh=mesh,
        in_specs=(P("ep", "dp", None), P("ep", "dp", None), P("ep", "dp", None), P(), P(), P()),
        out_specs=P(None, "ep", "dp", None),
        check_vma=False,
    )
```

profile of v0, /device:TPU:1, one launch (start us, length us, event | category | flops | bytes accessed | tf_op | source)
XLA Modules:
  0.0 143.5 jit_solution(5352892649726653841)
XLA Ops:
  0.0 0.9 convert_reduce_fusion.2
  0.9 0.6 select_reduce_fusion.1.refs_in_0_
  1.6 1.3 convert_reduce_fusion
  2.8 0.7 multiply_add_fusion
  3.5 1.4 %select_reduce_fusion = s32[1024]{0:T(1024)S(1)} fusion(s32[1024]{0:T(1024)S(1)} %multiply_add_fusion, s32[1024]{0:T(1024)} %param.10), kind=kLoop, calls=%fused_computation | loop fusion | flops 3144704 | bytes 12288 | tf_op jit(solution)/shard_map/reduce_sum | solution.py:23
  5.0 0.0 copy-start
  5.1 0.4 convert_reduce_fusion.1
  5.4 0.6 dynamic-slice_add_fusion.refs_in_1_
  6.0 0.1 add_bitcast_fusion
  6.1 0.6 copy.9
  6.7 0.0 copy-done
  6.7 131.5 %shard_map.64 = bf16[3,8,32,3584]{3,2,1,0:T(8,128)(2,1)} custom-call(s32[8]{0:T(128)} %select_reduce_fusion.1.refs_in_0_, s32[1,256]{1,0:T(1,128)} %dynamic-slice_add_fusion.refs_in_1_, s32[1,1024]{1,0:T(1,128)} %bitcast.15, s32[1,1024]{1,0:T(1,128)} %bitcast.16, f32[256,3584]{1,0:T(8,128)} %bitcast.12, f32[256,3584]{1,0:T(8,128)} %bitcast.13, ...), custom_call_target="tpu_custom_call" | custom-call | tf_op jit(solution)/shard_map/pallas_call | solution.py:276
  138.2 5.4 %copy.11 = bf16[3,1,256,3584]{3,2,1,0:T(8,128)(2,1)} copy(bf16[3,1,256,3584]{3,2,1,0:T(8,128)(2,1)} %bitcast.11) | data formatting | bytes 11010048
  (4 shorter events, 0.0 us)
Async XLA Ops:
  5.0 1.7 %copy-start = (s32[1024]{0:T(1024)}, s32[1024]{0:T(1024)S(1)}, u32[]{:S(2)}) copy-start(s32[1024]{0:T(1024)S(1)} %select_reduce_fusion) | copy-start | bytes 12292
where the time goes:
time: 144 us
  Pallas kernels  131 us (91%)
  other arithmetic  6.06 us (4%)
  local copies, waits for them, and re-layouts  5.98 us (4%)
    pallas_call x1, Pallas kernels, exchange(): pl.pallas_call(functools.partial(exchange_kernel, n_ep, n_dp, half), out_...  131 us
    unnamed x4, local copies, waits for them, and re-layouts  5.97 us

commit v1 on v0

--- a/solution.py
+++ b/solution.py
@@ -145,11 +145,10 @@
             copy.wait_recv()
 
     def own_out(c):
-        own = pl.ds(ep * m_ep, m_ep)
-        return pltpu.make_async_copy(sel.at[c, ep], out_ref.at[c, own, :, first], store.at[c])
+        out_ref[c, pl.ds(ep * m_ep, m_ep), :, first] = sel[c, ep]
 
     def placed_out(c):
-        return pltpu.make_async_copy(placed.at[c], out_ref.at[c - FIELDS, :, :, last], store.at[c])
+        out_ref[c - FIELDS, :, :, last] = placed[c]
 
     def sort(c):
         load_copy(c).wait()
@@ -205,7 +204,7 @@
             sel[c, k] = e1[c][order_ref[k]]
         start(b_copies(c))
         if c < FIELDS:
-            own_out(c).start()
+            own_out(c)
         else:
             mid[c, pl.ds(ep * m_ep, m_ep)] = sel[c, ep]
 
@@ -221,7 +220,7 @@
     def finish(c):
         arrive(z_copies(c))
         place(c, late.at[c - FIELDS])
-        placed_out(c).start()
+        placed_out(c)
 
     if aligned:
         before[...] = one_hot(position_ref, 0, rows)
@@ -259,7 +258,6 @@
         for copies in (z_copies(c), a_copies(c), b_copies(c)):
             for copy in copies:
                 copy.wait_send()
-        (own_out if c < FIELDS else placed_out)(c).wait()
 
 
 def exchange(order, indices, arrays, n_ep, n_dp):
@@ -275,9 +273,9 @@
     square = (rows, rows) if depth % 16 == 0 else (blocks, blocks, depth, depth)
     return pl.pallas_call(
         functools.partial(exchange_kernel, n_ep, n_dp, half),
-        out_shape=jax.ShapeDtypeStruct((FIELDS, blocks, depth, cols), bf16),
+        out_shape=pltpu.VMEM((FIELDS, blocks, depth, cols), bf16),
         in_specs=[pl.BlockSpec(memory_space=pltpu.SMEM), vmem, vmem, vmem] + [anywhere] * FIELDS,
-        out_specs=anywhere,
+        out_specs=vmem,
         scratch_shapes=[pltpu.VMEM((n_ep, per, depth, half), bf16)] * chunks
         + [
             pltpu.VMEM((chunks, rows, half), jnp.float32),
@@ -297,7 +295,7 @@
             dma((chunks, n_ep)),
             dma((chunks,)),
         ],
-        compiler_params=pltpu.CompilerParams(collective_id=0, has_side_effects=True),
+        compiler_params=pltpu.CompilerParams(collective_id=0, has_side_effects=True, vmem_limit_bytes=54 * 2**20),
     )(order, *indices, *arrays)
 
 

time: 144 us -> 140 us (0.972)
  local copies, waits for them, and re-layouts: 5.98 us -> 3.06 us
    unnamed x4, local copies, waits for them, and re-layouts: 5.97 us -> 3.05 us
where the time goes in v1:
time: 140 us
  Pallas kernels  131 us (94%)
  other arithmetic  6.07 us (4%)
  local copies, waits for them, and re-layouts  3.06 us (2%)
    pallas_call x1, Pallas kernels, exchange(): pl.pallas_call(functools.partial(exchange_kernel, n_ep, n_dp, half), out_...  131 us
    unnamed x4, local copies, waits for them, and re-layouts  3.05 us

profile of v1, /device:TPU:1, one launch (start us, length us, event | category | flops | bytes accessed | tf_op | source)
XLA Modules:
  0.0 139.8 jit_solution(14572661110228914311)
XLA Ops:
  0.0 0.9 convert_reduce_fusion.2
  0.9 0.7 select_reduce_fusion.1.refs_in_0_
  1.6 1.3 convert_reduce_fusion
  2.9 0.7 multiply_add_fusion
  3.5 1.4 %select_reduce_fusion = s32[1024]{0:T(1024)S(1)} fusion(s32[1024]{0:T(1024)S(1)} %multiply_add_fusion, s32[1024]{0:T(1024)} %param.10), kind=kLoop, calls=%fused_computation | loop fusion | flops 3144704 | bytes 12288 | tf_op jit(solution)/shard_map/reduce_sum | solution.py:23
  5.0 0.0 copy-start
  5.1 0.4 convert_reduce_fusion.1
  5.5 0.6 dynamic-slice_add_fusion.refs_in_1_
  6.1 0.1 add_bitcast_fusion
  6.1 0.6 copy.9
  6.7 0.0 copy-done
  6.7 130.7 %shard_map.64 = bf16[3,8,32,3584]{3,2,1,0:T(8,128)(2,1)S(1)} custom-call(s32[8]{0:T(128)} %select_reduce_fusion.1.refs_in_0_, s32[1,256]{1,0:T(1,128)} %dynamic-slice_add_fusion.refs_in_1_, s32[1,1024]{1,0:T(1,128)} %bitcast.15, s32[1,1024]{1,0:T(1,128)} %bitcast.16, f32[256,3584]{1,0:T(8,128)} %bitcast.12, f32[256,3584]{1,0:T(8,128)} %bitcast.13, ...), custom_call_target="tpu_custom_call" | custom-call | tf_op jit(solution)/shard_map/pallas_call | solution.py:274
  137.4 2.4 %copy.11 = bf16[3,1,256,3584]{3,2,1,0:T(8,128)(2,1)} copy(bf16[3,1,256,3584]{3,2,1,0:T(8,128)(2,1)S(1)} %bitcast.11) | data formatting | bytes 11010048
  (4 shorter events, 0.0 us)
Async XLA Ops:
  5.0 1.7 %copy-start = (s32[1024]{0:T(1024)}, s32[1024]{0:T(1024)S(1)}, u32[]{:S(2)}) copy-start(s32[1024]{0:T(1024)S(1)} %select_reduce_fusion) | copy-start | bytes 12292

commit v2 on v1

v2 whole, which is shorter than its diff:
```python
import functools
import math

import jax
import jax.numpy as jnp
from jax import lax
from jax.experimental import pallas as pl
from jax.experimental.pallas import tpu as pltpu
from jax.sharding import PartitionSpec as P

MESH = pl.DeviceIdType.MESH
FIELDS = 3
PACK = 16
BF16, F32, I32 = jnp.bfloat16, jnp.float32, jnp.int32


def cut(total, parts):
    units = total // 128
    return 128 * min(max(round(units * parts), 1), units - 1)


def widths(cols):
    if cols % 128:
        return [cols // 2] * FIELDS
    return [cut(cols, 2 / 7), cut(cols, 1 / 2), cut(cols, 5 / 7)]


def as_bf16(mask):
    return mask.astype(F32).astype(BF16)


def dot(left, right):
    return jnp.dot(left, right, preferred_element_type=F32)


def iota(shape, axis):
    return lax.broadcasted_iota(I32, shape, axis)


def one_hot(index_ref, first, depth):
    return as_bf16(index_ref[...] == iota((depth, index_ref.shape[1]), 0) + first)


def row_of(stack, row):
    return jnp.sum(jnp.where(iota(stack.shape, 0) == row, stack, 0.0), axis=0, keepdims=True)


def stack_rows(rows, width):
    out = jnp.zeros((PACK, width), F32)
    for i, row in enumerate(rows):
        out = jnp.where(iota((PACK, width), 0) == i, row, out)
    return out.astype(BF16)


def column_tiles(cols, body):
    tile = next((t for t in (512, 256, 128) if cols % t == 0), cols)

    @pl.loop(0, cols // tile)
    def _(i):
        body(pl.ds(pl.multiple_of(i * tile, tile), tile))


def partner(me, offset, n):
    out, bit = 0, 1
    while bit < n:
        out = out + ((me // bit + (offset // bit) % 2) % 2) * bit
        bit *= 2
    return out


def exchange_kernel(n_ep, n_dp, split, *refs_in):
    ids_ref, offsets_ref, writers_ref = refs_in[:3]
    fields_in, out_ref, scratch = refs_in[3 : 3 + FIELDS], refs_in[3 + FIELDS], list(refs_in[4 + FIELDS :])

    def take(count):
        head = scratch[:count]
        del scratch[:count]
        return head

    chunks = 2 * FIELDS
    wide, ready, mid, e1, sel = (take(chunks) for _ in range(5))
    placed, early, late = take(FIELDS), take(FIELDS), take(FIELDS)
    order_ref, position_ref, target_ref, arrives_ref, before, after, ahead = take(7)
    load, z_send, z_recv, a_send, a_recv, b_send, b_recv = scratch
    ep, dp = lax.axis_index("ep"), lax.axis_index("dp")
    _, blocks, depth, cols = out_ref.shape
    rows = blocks * depth
    total = offsets_ref.shape[1]
    pair = rows // n_dp
    aligned = depth % PACK == 0
    m_ep, m_dp = blocks // n_ep, blocks // n_dp
    z_order = sorted(range(1, n_dp), key=lambda o: (o == 1, o))
    e_order = sorted(range(1, n_ep), key=lambda o: (o == 1, o % 2, -o))

    def span(c):
        f = c % FIELDS
        return pl.ds(0, split[f]) if c < FIELDS else pl.ds(split[f], cols - split[f])

    def load_copy(c):
        return pltpu.make_async_copy(fields_in[c % FIELDS].at[:, span(c)], wide[c], load.at[c])

    turns = [c for f in range(FIELDS) for c in (f, FIELDS + f)]
    for c in turns:
        load_copy(c).start()

    barrier = pltpu.get_barrier_semaphore()
    for o in range(1, n_dp):
        pl.semaphore_signal(barrier, inc=1, device_id={"dp": partner(dp, o, n_dp)}, device_id_type=MESH)
    for o in range(1, n_ep):
        pl.semaphore_signal(barrier, inc=1, device_id={"ep": partner(ep, o, n_ep)}, device_id_type=MESH)

    def remote(src, dst, send, recv, axis, peer):
        return pltpu.make_async_remote_copy(
            src_ref=src, dst_ref=dst, send_sem=send, recv_sem=recv,
            device_id={axis: peer}, device_id_type=MESH,
        )

    def z_refs(c):
        return (ready[c], mid[c]) if c < FIELDS else (early[c - FIELDS], late[c - FIELDS])

    def a_ref(c):
        return placed[c] if c < FIELDS else ready[c]

    def b_ref(c):
        return out_ref.at[c, :, :, span(c)] if c < FIELDS else mid[c]

    def z_copies(c):
        src, dst = z_refs(c)
        return [
            remote(
                src.at[pl.ds(partner(dp, o, n_dp) * m_dp, m_dp)], dst.at[pl.ds(dp * m_dp, m_dp)],
                z_send.at[c, o], z_recv.at[c, o], "dp", partner(dp, o, n_dp),
            )
            for o in z_order
        ]

    def a_copies(c):
        return [
            remote(
                a_ref(c).at[pl.ds(partner(ep, o, n_ep) * m_ep, m_ep)], e1[c].at[ep],
                a_send.at[c, o], a_recv.at[c, o], "ep", partner(ep, o, n_ep),
            )
            for o in e_order
        ]

    def b_copies(c):
        return [
            remote(
                sel[c].at[partner(ep, o, n_ep)], b_ref(c).at[pl.ds(ep * m_ep, m_ep)],
                b_send.at[c, o], b_recv.at[c, o], "ep", partner(ep, o, n_ep),
            )
            for o in e_order
        ]

    def start(copies):
        for copy in copies:
            copy.start()

    def arrive(copies):
        for copy in copies:
            copy.wait_recv()

    def make_order():
        @pl.loop(0, n_ep)
        def _(k):
            def rank_of(e):
                def count(f, rank):
                    tied = (ids_ref[f] == ids_ref[e]) & (f < e)
                    return rank + ((ids_ref[f] < ids_ref[e]) | tied).astype(I32)

                return lax.fori_loop(0, n_ep, count, jnp.int32(0))

            order_ref[k] = lax.fori_loop(
                0, n_ep, lambda e, r: r + jnp.where(rank_of(e) == k, e, 0), jnp.int32(0)
            )

    def groups_of(writer):
        return (writer == iota((PACK, writer.shape[1]), 0).astype(writer.dtype)).astype(F32)

    def rank_in(groups):
        return dot(groups.astype(BF16), ahead[...])

    def pick(table, s):
        offsets = offsets_ref[:, pl.ds(pl.multiple_of(s * rows, rows), rows)]
        return dot(table, as_bf16(offsets == iota((total, rows), 0)))

    def writer_and_rank(writer):
        groups = groups_of(writer)
        return jnp.sum(groups * rank_in(groups), axis=0, keepdims=True)

    def make_position():
        ahead[...] = as_bf16(iota((rows, rows), 0) < iota((rows, rows), 1))
        picked = pick(stack_rows([writers_ref[...].astype(F32)], total), dp)
        writer = row_of(picked, 0)
        position_ref[...] = (writer * pair + writer_and_rank(writer)).astype(I32)

    def make_targets():
        carry = jnp.zeros((PACK, 1), F32)
        within = []
        for s in range(n_dp):
            groups = groups_of(writers_ref[:, s * rows : (s + 1) * rows])
            count = rank_in(groups) + carry
            carry = carry + jnp.sum(groups, axis=1, keepdims=True)
            within.append(jnp.sum(groups * count, axis=0, keepdims=True).astype(I32))
        place = jnp.concatenate(within, axis=1)
        table = stack_rows(
            [writers_ref[...].astype(F32), (place // 256).astype(F32), (place % 256).astype(F32)], total
        )

        @pl.loop(0, n_dp)
        def _(s):
            picked = pick(table, s)
            writer = row_of(picked, 0)
            here = pl.ds(pl.multiple_of(s * rows, rows), rows)
            target_ref[:, here] = (writer * rows + row_of(picked, 1) * 256 + row_of(picked, 2)).astype(I32)
            arrives_ref[:, here] = (writer_and_rank(writer)).astype(I32) + s * pair

    def after_of(i, j, size):
        return lax.dot_general(
            one_hot(target_ref, dp * rows + i * size, size), one_hot(arrives_ref, j * size, size),
            (((1,), (1,)), ((), ())), preferred_element_type=F32,
        ).astype(BF16)

    def permute(matrix, src, dst):
        def body(part):
            if aligned:
                x = src[:, :, part].reshape(rows, part.size)
                dst[:, :, part] = dot(matrix[...], x).astype(BF16).reshape(blocks, depth, part.size)
            else:
                @pl.loop(0, blocks)
                def _(i):
                    def add(j, so_far):
                        return so_far + dot(matrix[i, j], src[j, :, part])

                    dst[i, :, part] = lax.fori_loop(
                        0, blocks, add, jnp.zeros((depth, part.size), F32)
                    ).astype(BF16)

        column_tiles(dst.shape[2], body)

    def sort(c):
        load_copy(c).wait()

        def body(part):
            x = wide[c][:, part].astype(BF16)
            if aligned:
                ready[c][:, :, part] = dot(before[...], x).astype(BF16).reshape(blocks, depth, part.size)
            else:
                @pl.loop(0, blocks)
                def _(i):
                    ready[c][i, :, part] = dot(one_hot(position_ref, i * depth, depth), x).astype(BF16)

        column_tiles(ready[c].shape[2], body)

    def narrow(c):
        load_copy(c).wait()

        def body(part):
            x = wide[c][:, part].astype(BF16)
            if aligned:
                ready[c][:, :, part] = x.reshape(blocks, depth, part.size)
            else:
                @pl.loop(0, blocks)
                def _(i):
                    keep = as_bf16(iota((depth, rows), 0) + i * depth == iota((depth, rows), 1))
                    ready[c][i, :, part] = dot(keep, x).astype(BF16)

        column_tiles(ready[c].shape[2], body)

    def z_start(c):
        start(z_copies(c))
        src, dst = z_refs(c)
        own = pl.ds(dp * m_dp, m_dp)
        dst[own] = src[own]

    def a_start(c):
        start(a_copies(c))
        e1[c][ep] = a_ref(c)[pl.ds(ep * m_ep, m_ep)]

    def a_to_b(c):
        arrive(a_copies(c))
        for k in range(n_ep):
            sel[c][k] = e1[c][order_ref[k]]
        start(b_copies(c))
        b_ref(c)[pl.ds(ep * m_ep, m_ep)] = sel[c][ep]

    def z_to_a(c):
        arrive(z_copies(c))
        permute(after, mid[c], placed[c])
        a_start(c)

    def b_to_z(c):
        arrive(b_copies(c))
        permute(before, mid[c], early[c - FIELDS])
        z_start(c)

    def finish(c):
        arrive(z_copies(c))
        permute(after, late[c - FIELDS], out_ref.at[c - FIELDS, :, :, span(c)])

    make_position()
    if aligned:
        before[...] = one_hot(position_ref, 0, rows)
    sort(0)
    pl.semaphore_wait(barrier, n_dp + n_ep - 2)
    z_start(0)
    narrow(3)
    a_start(3)
    for f in range(1, FIELDS):
        sort(f)
        z_start(f)
        narrow(FIELDS + f)
        a_start(FIELDS + f)
    make_order()
    make_targets()
    if aligned:
        after[...] = after_of(0, 0, rows)
    else:
        @pl.loop(0, blocks)
        def _(i):
            @pl.loop(0, blocks)
            def _(j):
                after[i, j] = after_of(i, j, depth)
                mine = as_bf16(position_ref[...] == iota((depth, rows), 0) + i * depth)
                whose = as_bf16(iota((depth, rows), 1) == iota((depth, rows), 0) + j * depth)
                before[i, j] = lax.dot_general(
                    mine, whose, (((1,), (1,)), ((), ())), preferred_element_type=F32
                ).astype(BF16)
    z_to_a(0)
    a_to_b(3)
    a_to_b(4)
    a_to_b(5)
    z_to_a(1)
    a_to_b(0)
    b_to_z(3)
    z_to_a(2)
    b_to_z(4)
    b_to_z(5)
    a_to_b(1)
    finish(3)
    a_to_b(2)
    finish(4)
    arrive(b_copies(0))
    arrive(b_copies(1))
    finish(5)
    arrive(b_copies(2))
    for c in range(chunks):
        for copies in (z_copies(c), a_copies(c), b_copies(c)):
            for copy in copies:
                copy.wait_send()


def exchange(expert_ids, offsets, writers, arrays, n_ep, n_dp):
    rows, cols = arrays[0].shape
    total = offsets.shape[1]
    depth = math.gcd(rows // n_dp, rows // n_ep)
    blocks = rows // depth
    split = widths(cols)
    per = blocks // n_ep
    size = split + [cols - w for w in split]
    dma = pltpu.SemaphoreType.DMA
    vmem = pl.BlockSpec(memory_space=pltpu.VMEM)
    square = (rows, rows) if depth % PACK == 0 else (blocks, blocks, depth, depth)

    def each(shape, widths_of, kind=BF16):
        return [pltpu.VMEM((*shape, w), kind) for w in widths_of]

    first, last = size[:FIELDS], size[FIELDS:]
    chunks = 2 * FIELDS
    return pl.pallas_call(
        functools.partial(exchange_kernel, n_ep, n_dp, split),
        out_shape=pltpu.VMEM((FIELDS, blocks, depth, cols), BF16),
        in_specs=[pl.BlockSpec(memory_space=pltpu.SMEM), vmem, vmem] + [pl.BlockSpec(memory_space=pl.ANY)] * FIELDS,
        out_specs=vmem,
        scratch_shapes=each((rows,), size, F32)
        + each((blocks, depth), size)
        + each((blocks, depth), size)
        + each((n_ep, per, depth), size)
        + each((n_ep, per, depth), size)
        + each((blocks, depth), first)
        + each((blocks, depth), last)
        + each((blocks, depth), last)
        + [
            pltpu.SMEM((n_ep,), I32),
            pltpu.VMEM((1, rows), I32),
            pltpu.VMEM((1, total), I32),
            pltpu.VMEM((1, total), I32),
            pltpu.VMEM(square, BF16),
            pltpu.VMEM(square, BF16),
            pltpu.VMEM((rows, rows), BF16),
            dma((chunks,)),
            dma((chunks, n_dp)),
            dma((chunks, n_dp)),
            dma((chunks, n_ep)),
            dma((chunks, n_ep)),
            dma((chunks, n_ep)),
            dma((chunks, n_ep)),
        ],
        compiler_params=pltpu.CompilerParams(
            collective_id=0, has_side_effects=True, vmem_limit_bytes=54 * 2**20
        ),
    )(expert_ids, offsets, writers, *arrays)


def on_device(master_weights, first_moment, second_moment, expert_ids, bucket_offsets, writer_rank):
    n_dp, n_ep = lax.axis_size("dp"), lax.axis_size("ep")
    _, rows, cols = master_weights.shape
    total = bucket_offsets.shape[0]
    arrays = (master_weights[0], first_moment[0], second_moment[0])
    saved = exchange(
        expert_ids, bucket_offsets.reshape(1, total), writer_rank.reshape(1, total), arrays, n_ep, n_dp
    )
    return saved.reshape(FIELDS, 1, rows, cols)


def solution(mesh):
    return jax.shard_map(
        on_device,
        mesh=mesh,
        in_specs=(P("ep", "dp", None), P("ep", "dp", None), P("ep", "dp", None), P(), P(), P()),
        out_specs=P(None, "ep", "dp", None),
        check_vma=False,
    )
```

time: 140 us -> 130 us (0.929)
  other arithmetic: 6.07 us -> 0 us
  Pallas kernels: 131 us -> 128 us
    reduce_sum x5 -> x0, other arithmetic: 4.68 us -> none  [the longest x1 1.45 us: tables(): jnp.sum(jnp.where(bucket_offsets[:, None] == p[None, :], place[None, :],...]
    pallas_call x1, Pallas kernels: 131 us -> 128 us  [exchange(): pl.pallas_call(functools.partial(exchange_kernel, n_ep, n_dp, split), out...]
    unnamed x4 -> x1, local copies, waits for them, and re-layouts: 3.05 us -> 2.45 us
where the time goes in v2:
time: 130 us
  Pallas kernels  128 us (98%)
  local copies, waits for them, and re-layouts  2.45 us (2%)
    pallas_call x1, Pallas kernels, exchange(): pl.pallas_call(functools.partial(exchange_kernel, n_ep, n_dp, split), out...  128 us

profile of v2, /device:TPU:1, one launch (start us, length us, event | category | flops | bytes accessed | tf_op | source)
XLA Modules:
  0.0 130.2 jit_solution(7711407366223615275)
XLA Ops:
  0.0 127.8 %shard_map.64 = bf16[3,8,32,3584]{3,2,1,0:T(8,128)(2,1)S(1)} custom-call(s32[8]{0:T(128)} %refs_in_0_.1, s32[1,1024]{1,0:T(1,128)} %bitcast.12, s32[1,1024]{1,0:T(1,128)} %bitcast.13, f32[256,3584]{1,0:T(8,128)} %bitcast.9, f32[256,3584]{1,0:T(8,128)} %bitcast.10, f32[256,3584]{1,0:T(8,128)} %bitcast.11), custom_call_target="tpu_custom_call" | custom-call | tf_op jit(solution)/shard_map/pallas_call | solution.py:370
  127.8 2.4 %copy.9 = bf16[3,1,256,3584]{3,2,1,0:T(8,128)(2,1)} copy(bf16[3,1,256,3584]{3,2,1,0:T(8,128)(2,1)S(1)} %bitcast.8) | data formatting | bytes 11010048

commit v3 on v2

--- a/solution.py
+++ b/solution.py
@@ -69,7 +69,7 @@
 
 
 def exchange_kernel(n_ep, n_dp, split, *refs_in):
-    ids_ref, offsets_ref, writers_ref = refs_in[:3]
+    indices_in = refs_in[:3]
     fields_in, out_ref, scratch = refs_in[3 : 3 + FIELDS], refs_in[3 + FIELDS], list(refs_in[4 + FIELDS :])
 
     def take(count):
@@ -80,16 +80,21 @@
     chunks = 2 * FIELDS
     wide, ready, mid, e1, sel = (take(chunks) for _ in range(5))
     placed, early, late = take(FIELDS), take(FIELDS), take(FIELDS)
-    order_ref, position_ref, target_ref, arrives_ref, before, after, ahead = take(7)
-    load, z_send, z_recv, a_send, a_recv, b_send, b_recv = scratch
+    ids_ref, offsets_ref, writers_ref = take(3)
+    rank_ref, order_ref, position_ref, target_ref, arrives_ref, before, after, ahead = take(8)
+    load, z_send, z_recv, a_send, a_recv, b_send, b_recv, index_load, told = scratch
     ep, dp = lax.axis_index("ep"), lax.axis_index("dp")
     _, blocks, depth, cols = out_ref.shape
     rows = blocks * depth
     total = offsets_ref.shape[1]
+    index_copies = [
+        pltpu.make_async_copy(src, dst, index_load.at[i])
+        for i, (src, dst) in enumerate(zip(indices_in, (ids_ref, offsets_ref, writers_ref), strict=True))
+    ]
     pair = rows // n_dp
     aligned = depth % PACK == 0
     m_ep, m_dp = blocks // n_ep, blocks // n_dp
-    z_order = sorted(range(1, n_dp), key=lambda o: (o == 1, o))
+    z_order = sorted(range(1, n_dp))
     e_order = sorted(range(1, n_ep), key=lambda o: (o == 1, o % 2, -o))
 
     def span(c):
@@ -99,15 +104,49 @@
     def load_copy(c):
         return pltpu.make_async_copy(fields_in[c % FIELDS].at[:, span(c)], wide[c], load.at[c])
 
-    turns = [c for f in range(FIELDS) for c in (f, FIELDS + f)]
-    for c in turns:
+
+    for copy in index_copies:
+        copy.start()
+    load_copy(5).start()
+    load_copy(0).start()
+
+    barrier = pltpu.get_barrier_semaphore()
+    even = ep % 2 == 0
+    odd_of_pair = ep + 1 - ep % 2
+    for o in range(1, n_dp):
+        pl.semaphore_signal(
+            barrier, inc=1, device_id={"dp": partner(dp, o, n_dp), "ep": odd_of_pair}, device_id_type=MESH
+        )
+    for o in range(1, n_ep):
+        @pl.when(partner(ep, o, n_ep) % 2 == 0)
+        def _(o=o):
+            pl.semaphore_signal(barrier, inc=1, device_id={"ep": partner(ep, o, n_ep)}, device_id_type=MESH)
+
+    for c in (3, 1, 4, 2):
         load_copy(c).start()
 
-    barrier = pltpu.get_barrier_semaphore()
-    for o in range(1, n_dp):
-        pl.semaphore_signal(barrier, inc=1, device_id={"dp": partner(dp, o, n_dp)}, device_id_type=MESH)
-    for o in range(1, n_ep):
-        pl.semaphore_signal(barrier, inc=1, device_id={"ep": partner(ep, o, n_ep)}, device_id_type=MESH)
+    def tell_partner():
+        pl.semaphore_signal(told, inc=1, device_id={"ep": partner(ep, 1, n_ep)}, device_id_type=MESH)
+
+    def ep_group_is_in():
+        @pl.when(even)
+        def _():
+            pl.semaphore_wait(barrier, n_ep - 1)
+            tell_partner()
+
+        @pl.when(jnp.logical_not(even))
+        def _():
+            pl.semaphore_wait(told, 1)
+
+    def dp_group_is_in():
+        @pl.when(jnp.logical_not(even))
+        def _():
+            pl.semaphore_wait(barrier, 2 * (n_dp - 1))
+            tell_partner()
+
+        @pl.when(even)
+        def _():
+            pl.semaphore_wait(told, 1)
 
     def remote(src, dst, send, recv, axis, peer):
         return pltpu.make_async_remote_copy(
@@ -129,7 +168,7 @@
         return [
             remote(
                 src.at[pl.ds(partner(dp, o, n_dp) * m_dp, m_dp)], dst.at[pl.ds(dp * m_dp, m_dp)],
-                z_send.at[c, o], z_recv.at[c, o], "dp", partner(dp, o, n_dp),
+                z_send.at[c], z_recv.at[c], "dp", partner(dp, o, n_dp),
             )
             for o in z_order
         ]
@@ -138,7 +177,7 @@
         return [
             remote(
                 a_ref(c).at[pl.ds(partner(ep, o, n_ep) * m_ep, m_ep)], e1[c].at[ep],
-                a_send.at[c, o], a_recv.at[c, o], "ep", partner(ep, o, n_ep),
+                a_send.at[c], a_recv.at[c], "ep", partner(ep, o, n_ep),
             )
             for o in e_order
         ]
@@ -147,32 +186,50 @@
         return [
             remote(
                 sel[c].at[partner(ep, o, n_ep)], b_ref(c).at[pl.ds(ep * m_ep, m_ep)],
-                b_send.at[c, o], b_recv.at[c, o], "ep", partner(ep, o, n_ep),
+                b_send.at[c], b_recv.at[c], "ep", partner(ep, o, n_ep),
             )
             for o in e_order
         ]
 
+    def z_all(c):
+        src, dst = z_refs(c)
+        part = pl.ds(0, (n_dp - 1) * m_dp)
+        return remote(src.at[part], dst.at[part], z_send.at[c], z_recv.at[c], "dp", partner(dp, 1, n_dp))
+
+    def a_all(c):
+        part = pl.ds(0, (n_ep - 1) * m_ep)
+        return remote(
+            a_ref(c).at[part], e1[c].at[pl.ds(0, n_ep - 1)], a_send.at[c], a_recv.at[c], "ep", partner(ep, 1, n_ep)
+        )
+
+    def b_all(c):
+        part = pl.ds(0, (n_ep - 1) * m_ep)
+        return remote(
+            sel[c].at[pl.ds(0, n_ep - 1)], b_ref(c).at[part], b_send.at[c], b_recv.at[c], "ep", partner(ep, 1, n_ep)
+        )
+
     def start(copies):
         for copy in copies:
             copy.start()
 
-    def arrive(copies):
-        for copy in copies:
-            copy.wait_recv()
-
     def make_order():
+        def rank_of(e):
+            rank = jnp.int32(0)
+            for f in range(n_ep):
+                tied = (ids_ref[f] == ids_ref[e]) & (f < e)
+                rank = rank + ((ids_ref[f] < ids_ref[e]) | tied).astype(I32)
+            return rank
+
+        @pl.loop(0, n_ep)
+        def _(e):
+            rank_ref[e] = rank_of(e)
+
         @pl.loop(0, n_ep)
         def _(k):
-            def rank_of(e):
-                def count(f, rank):
-                    tied = (ids_ref[f] == ids_ref[e]) & (f < e)
-                    return rank + ((ids_ref[f] < ids_ref[e]) | tied).astype(I32)
-
-                return lax.fori_loop(0, n_ep, count, jnp.int32(0))
-
-            order_ref[k] = lax.fori_loop(
-                0, n_ep, lambda e, r: r + jnp.where(rank_of(e) == k, e, 0), jnp.int32(0)
-            )
+            source = jnp.int32(0)
+            for e in range(n_ep):
+                source = source + jnp.where(rank_ref[e] == k, e, 0)
+            order_ref[k] = source
 
     def groups_of(writer):
         return (writer == iota((PACK, writer.shape[1]), 0).astype(writer.dtype)).astype(F32)
@@ -278,39 +335,54 @@
         e1[c][ep] = a_ref(c)[pl.ds(ep * m_ep, m_ep)]
 
     def a_to_b(c):
-        arrive(a_copies(c))
+        a_all(c).wait_recv()
         for k in range(n_ep):
             sel[c][k] = e1[c][order_ref[k]]
         start(b_copies(c))
         b_ref(c)[pl.ds(ep * m_ep, m_ep)] = sel[c][ep]
 
     def z_to_a(c):
-        arrive(z_copies(c))
+        z_all(c).wait_recv()
         permute(after, mid[c], placed[c])
         a_start(c)
 
+    def back(c):
+        b_all(c).wait_recv()
+        permute(before, mid[c], early[c - FIELDS])
+
     def b_to_z(c):
-        arrive(b_copies(c))
-        permute(before, mid[c], early[c - FIELDS])
+        back(c)
         z_start(c)
 
+    def z_to_a_and_z(c, following):
+        z_all(c).wait_recv()
+        z_start(following)
+        permute(after, mid[c], placed[c])
+        a_start(c)
+
     def finish(c):
-        arrive(z_copies(c))
+        z_all(c).wait_recv()
         permute(after, late[c - FIELDS], out_ref.at[c - FIELDS, :, :, span(c)])
 
+    narrow(5)
+    ep_group_is_in()
+    a_start(5)
+    for copy in index_copies:
+        copy.wait()
     make_position()
     if aligned:
         before[...] = one_hot(position_ref, 0, rows)
     sort(0)
-    pl.semaphore_wait(barrier, n_dp + n_ep - 2)
+    dp_group_is_in()
     z_start(0)
     narrow(3)
     a_start(3)
-    for f in range(1, FIELDS):
-        sort(f)
-        z_start(f)
-        narrow(FIELDS + f)
-        a_start(FIELDS + f)
+    sort(1)
+    z_start(1)
+    narrow(4)
+    a_start(4)
+    sort(2)
+    z_start(2)
     make_order()
     make_targets()
     if aligned:
@@ -326,28 +398,28 @@
                 before[i, j] = lax.dot_general(
                     mine, whose, (((1,), (1,)), ((), ())), preferred_element_type=F32
                 ).astype(BF16)
+    a_to_b(3)
     z_to_a(0)
-    a_to_b(3)
     a_to_b(4)
     a_to_b(5)
     z_to_a(1)
     a_to_b(0)
-    b_to_z(3)
-    z_to_a(2)
+    back(3)
+    z_to_a_and_z(2, 3)
     b_to_z(4)
     b_to_z(5)
     a_to_b(1)
     finish(3)
     a_to_b(2)
     finish(4)
-    arrive(b_copies(0))
-    arrive(b_copies(1))
+    b_all(0).wait_recv()
+    b_all(1).wait_recv()
     finish(5)
-    arrive(b_copies(2))
+    b_all(2).wait_recv()
     for c in range(chunks):
-        for copies in (z_copies(c), a_copies(c), b_copies(c)):
-            for copy in copies:
-                copy.wait_send()
+        z_all(c).wait_send()
+        a_all(c).wait_send()
+        b_all(c).wait_send()
 
 
 def exchange(expert_ids, offsets, writers, arrays, n_ep, n_dp):
@@ -370,7 +442,7 @@
     return pl.pallas_call(
         functools.partial(exchange_kernel, n_ep, n_dp, split),
         out_shape=pltpu.VMEM((FIELDS, blocks, depth, cols), BF16),
-        in_specs=[pl.BlockSpec(memory_space=pltpu.SMEM), vmem, vmem] + [pl.BlockSpec(memory_space=pl.ANY)] * FIELDS,
+        in_specs=[pl.BlockSpec(memory_space=pl.ANY)] * (3 + FIELDS),
         out_specs=vmem,
         scratch_shapes=each((rows,), size, F32)
         + each((blocks, depth), size)
@@ -382,6 +454,10 @@
         + each((blocks, depth), last)
         + [
             pltpu.SMEM((n_ep,), I32),
+            pltpu.VMEM((1, total), I32),
+            pltpu.VMEM((1, total), I32),
+            pltpu.SMEM((n_ep,), I32),
+            pltpu.SMEM((n_ep,), I32),
             pltpu.VMEM((1, rows), I32),
             pltpu.VMEM((1, total), I32),
             pltpu.VMEM((1, total), I32),
@@ -389,12 +465,14 @@
             pltpu.VMEM(square, BF16),
             pltpu.VMEM((rows, rows), BF16),
             dma((chunks,)),
-            dma((chunks, n_dp)),
-            dma((chunks, n_dp)),
-            dma((chunks, n_ep)),
-            dma((chunks, n_ep)),
-            dma((chunks, n_ep)),
-            dma((chunks, n_ep)),
+            dma((chunks,)),
+            dma((chunks,)),
+            dma((chunks,)),
+            dma((chunks,)),
+            dma((chunks,)),
+            dma((chunks,)),
+            dma((3,)),
+            pltpu.SemaphoreType.REGULAR,
         ],
         compiler_params=pltpu.CompilerParams(
             collective_id=0, has_side_effects=True, vmem_limit_bytes=54 * 2**20

time: 130 us -> 129 us (level); the launches traced: 130 us -> 127 us
  Pallas kernels: 128 us -> 125 us
    pallas_call x1, Pallas kernels: 128 us -> 125 us  [exchange(): pl.pallas_call(functools.partial(exchange_kernel, n_ep, n_dp, split), out...]
where the time goes in v3:
time: 129 us; the launch traced here: 127 us
  Pallas kernels  125 us (97%)
  local copies, waits for them, and re-layouts  2.45 us (2%)
    pallas_call x1, Pallas kernels, exchange(): pl.pallas_call(functools.partial(exchange_kernel, n_ep, n_dp, split), out...  125 us

profile of v3, /device:TPU:1, one launch (start us, length us, event | category | flops | bytes accessed | tf_op | source)
XLA Modules:
  0.0 127.3 jit_solution(1570691055344282799)
XLA Ops:
  0.0 124.9 %shard_map.64 = bf16[3,8,32,3584]{3,2,1,0:T(8,128)(2,1)S(1)} custom-call(s32[8]{0:T(128)} %refs_in_0_.1, s32[1,1024]{1,0:T(1,128)} %bitcast.12, s32[1,1024]{1,0:T(1,128)} %bitcast.13, f32[256,3584]{1,0:T(8,128)} %bitcast.9, f32[256,3584]{1,0:T(8,128)} %bitcast.10, f32[256,3584]{1,0:T(8,128)} %bitcast.11), custom_call_target="tpu_custom_call" | custom-call | tf_op jit(solution)/shard_map/pallas_call | solution.py:442
  124.9 2.4 %copy.9 = bf16[3,1,256,3584]{3,2,1,0:T(8,128)(2,1)} copy(bf16[3,1,256,3584]{3,2,1,0:T(8,128)(2,1)S(1)} %bitcast.8) | data formatting | bytes 11010048

commit v4 on v3

--- a/solution.py
+++ b/solution.py
@@ -68,9 +68,58 @@
     return out
 
 
+def permute_rows(aligned, matrix, src, dst):
+    blocks, depth, width = dst.shape
+    rows = blocks * depth
+
+    def body(part):
+        if aligned:
+            x = src[:, :, part].reshape(rows, part.size)
+            dst[:, :, part] = dot(matrix[...], x).astype(BF16).reshape(blocks, depth, part.size)
+        else:
+            @pl.loop(0, blocks)
+            def _(i):
+                def add(j, so_far):
+                    return so_far + dot(matrix[i, j], src[j, :, part])
+
+                dst[i, :, part] = lax.fori_loop(
+                    0, blocks, add, jnp.zeros((depth, part.size), F32)
+                ).astype(BF16)
+
+    column_tiles(width, body)
+
+
+def last_kernel(split, most_ref, late_ref, after_ref, out_ref, placed, store):
+    blocks, depth, cols = most_ref.shape[1:]
+    parts = 4 if blocks % 4 == 0 else 1
+    some = blocks // parts
+    f = FIELDS - 1
+
+    def copies(field, width):
+        return [
+            pltpu.make_async_copy(
+                most_ref.at[field, pl.ds(i * some, some), :, pl.ds(0, width)],
+                out_ref.at[field, pl.ds(i * some, some), :, pl.ds(0, width)],
+                store.at[field, i],
+            )
+            for i in range(parts)
+        ]
+
+    moves = [copy for field in range(FIELDS) for copy in copies(field, cols if field < f else split[f])]
+    for copy in moves:
+        copy.start()
+    permute_rows(depth % PACK == 0, after_ref, late_ref, placed)
+    rest = pltpu.make_async_copy(placed, out_ref.at[f, :, :, pl.ds(split[f], cols - split[f])], store.at[FIELDS, 0])
+    rest.start()
+    for copy in moves:
+        copy.wait()
+    rest.wait()
+
+
 def exchange_kernel(n_ep, n_dp, split, *refs_in):
     indices_in = refs_in[:3]
-    fields_in, out_ref, scratch = refs_in[3 : 3 + FIELDS], refs_in[3 + FIELDS], list(refs_in[4 + FIELDS :])
+    fields_in, out_ref, scratch = refs_in[3 : 3 + FIELDS], refs_in[3 + FIELDS], list(refs_in[6 + FIELDS :])
+    last_late, after = refs_in[4 + FIELDS : 6 + FIELDS]
 
     def take(count):
         head = scratch[:count]
@@ -79,10 +128,10 @@
 
     chunks = 2 * FIELDS
     wide, ready, mid, e1, sel = (take(chunks) for _ in range(5))
-    placed, early, late = take(FIELDS), take(FIELDS), take(FIELDS)
+    placed, early, late = take(FIELDS), take(FIELDS), take(FIELDS - 1) + [last_late]
     ids_ref, offsets_ref, writers_ref = take(3)
-    rank_ref, order_ref, position_ref, target_ref, arrives_ref, before, after, ahead = take(8)
-    load, z_send, z_recv, a_send, a_recv, b_send, b_recv, index_load, told = scratch
+    rank_ref, order_ref, position_ref, target_ref, arrives_ref, before, ahead = take(7)
+    load, z_send, z_recv, a_send, a_recv, b_send, b_recv, index_load = scratch
     ep, dp = lax.axis_index("ep"), lax.axis_index("dp")
     _, blocks, depth, cols = out_ref.shape
     rows = blocks * depth
@@ -111,42 +160,13 @@
     load_copy(0).start()
 
     barrier = pltpu.get_barrier_semaphore()
-    even = ep % 2 == 0
-    odd_of_pair = ep + 1 - ep % 2
     for o in range(1, n_dp):
-        pl.semaphore_signal(
-            barrier, inc=1, device_id={"dp": partner(dp, o, n_dp), "ep": odd_of_pair}, device_id_type=MESH
-        )
+        pl.semaphore_signal(barrier, inc=1, device_id={"dp": partner(dp, o, n_dp)}, device_id_type=MESH)
     for o in range(1, n_ep):
-        @pl.when(partner(ep, o, n_ep) % 2 == 0)
-        def _(o=o):
-            pl.semaphore_signal(barrier, inc=1, device_id={"ep": partner(ep, o, n_ep)}, device_id_type=MESH)
+        pl.semaphore_signal(barrier, inc=1, device_id={"ep": partner(ep, o, n_ep)}, device_id_type=MESH)
 
     for c in (3, 1, 4, 2):
         load_copy(c).start()
-
-    def tell_partner():
-        pl.semaphore_signal(told, inc=1, device_id={"ep": partner(ep, 1, n_ep)}, device_id_type=MESH)
-
-    def ep_group_is_in():
-        @pl.when(even)
-        def _():
-            pl.semaphore_wait(barrier, n_ep - 1)
-            tell_partner()
-
-        @pl.when(jnp.logical_not(even))
-        def _():
-            pl.semaphore_wait(told, 1)
-
-    def dp_group_is_in():
-        @pl.when(jnp.logical_not(even))
-        def _():
-            pl.semaphore_wait(barrier, 2 * (n_dp - 1))
-            tell_partner()
-
-        @pl.when(even)
-        def _():
-            pl.semaphore_wait(told, 1)
 
     def remote(src, dst, send, recv, axis, peer):
         return pltpu.make_async_remote_copy(
@@ -278,22 +298,7 @@
             (((1,), (1,)), ((), ())), preferred_element_type=F32,
         ).astype(BF16)
 
-    def permute(matrix, src, dst):
-        def body(part):
-            if aligned:
-                x = src[:, :, part].reshape(rows, part.size)
-                dst[:, :, part] = dot(matrix[...], x).astype(BF16).reshape(blocks, depth, part.size)
-            else:
-                @pl.loop(0, blocks)
-                def _(i):
-                    def add(j, so_far):
-                        return so_far + dot(matrix[i, j], src[j, :, part])
-
-                    dst[i, :, part] = lax.fori_loop(
-                        0, blocks, add, jnp.zeros((depth, part.size), F32)
-                    ).astype(BF16)
-
-        column_tiles(dst.shape[2], body)
+    permute = functools.partial(permute_rows, aligned)
 
     def sort(c):
         load_copy(c).wait()
@@ -346,34 +351,24 @@
         permute(after, mid[c], placed[c])
         a_start(c)
 
-    def back(c):
+    def b_to_z(c):
         b_all(c).wait_recv()
         permute(before, mid[c], early[c - FIELDS])
-
-    def b_to_z(c):
-        back(c)
         z_start(c)
-
-    def z_to_a_and_z(c, following):
-        z_all(c).wait_recv()
-        z_start(following)
-        permute(after, mid[c], placed[c])
-        a_start(c)
 
     def finish(c):
         z_all(c).wait_recv()
         permute(after, late[c - FIELDS], out_ref.at[c - FIELDS, :, :, span(c)])
 
     narrow(5)
-    ep_group_is_in()
-    a_start(5)
     for copy in index_copies:
         copy.wait()
     make_position()
     if aligned:
         before[...] = one_hot(position_ref, 0, rows)
     sort(0)
-    dp_group_is_in()
+    pl.semaphore_wait(barrier, n_dp + n_ep - 2)
+    a_start(5)
     z_start(0)
     narrow(3)
     a_start(3)
@@ -404,17 +399,17 @@
     a_to_b(5)
     z_to_a(1)
     a_to_b(0)
-    back(3)
-    z_to_a_and_z(2, 3)
+    b_to_z(3)
+    z_to_a(2)
     b_to_z(4)
     b_to_z(5)
     a_to_b(1)
+    a_to_b(2)
     finish(3)
-    a_to_b(2)
     finish(4)
     b_all(0).wait_recv()
     b_all(1).wait_recv()
-    finish(5)
+    z_all(5).wait_recv()
     b_all(2).wait_recv()
     for c in range(chunks):
         z_all(c).wait_send()
@@ -439,11 +434,15 @@
 
     first, last = size[:FIELDS], size[FIELDS:]
     chunks = 2 * FIELDS
-    return pl.pallas_call(
+    most, late, after = pl.pallas_call(
         functools.partial(exchange_kernel, n_ep, n_dp, split),
-        out_shape=pltpu.VMEM((FIELDS, blocks, depth, cols), BF16),
+        out_shape=[
+            pltpu.VMEM((FIELDS, blocks, depth, cols), BF16),
+            pltpu.VMEM((blocks, depth, last[-1]), BF16),
+            pltpu.VMEM(square, BF16),
+        ],
         in_specs=[pl.BlockSpec(memory_space=pl.ANY)] * (3 + FIELDS),
-        out_specs=vmem,
+        out_specs=[vmem] * 3,
         scratch_shapes=each((rows,), size, F32)
         + each((blocks, depth), size)
         + each((blocks, depth), size)
@@ -451,7 +450,7 @@
         + each((n_ep, per, depth), size)
         + each((blocks, depth), first)
         + each((blocks, depth), last)
-        + each((blocks, depth), last)
+        + each((blocks, depth), last[:-1])
         + [
             pltpu.SMEM((n_ep,), I32),
             pltpu.VMEM((1, total), I32),
@@ -462,7 +461,6 @@
             pltpu.VMEM((1, total), I32),
             pltpu.VMEM((1, total), I32),
             pltpu.VMEM(square, BF16),
-            pltpu.VMEM(square, BF16),
             pltpu.VMEM((rows, rows), BF16),
             dma((chunks,)),
             dma((chunks,)),
@@ -472,12 +470,20 @@
             dma((chunks,)),
             dma((chunks,)),
             dma((3,)),
-            pltpu.SemaphoreType.REGULAR,
         ],
         compiler_params=pltpu.CompilerParams(
             collective_id=0, has_side_effects=True, vmem_limit_bytes=54 * 2**20
         ),
     )(expert_ids, offsets, writers, *arrays)
+    in_vmem = [pltpu.with_memory_space_constraint(x, pltpu.VMEM) for x in (most, late, after)]
+    return pl.pallas_call(
+        functools.partial(last_kernel, split),
+        out_shape=jax.ShapeDtypeStruct((FIELDS, blocks, depth, cols), BF16),
+        in_specs=[vmem] * 3,
+        out_specs=pl.BlockSpec(memory_space=pl.ANY),
+        scratch_shapes=[pltpu.VMEM((blocks, depth, last[-1]), BF16), dma((FIELDS + 1, 4))],
+        compiler_params=pltpu.CompilerParams(vmem_limit_bytes=8 * 2**20),
+    )(*in_vmem)
 
 
 def on_device(master_weights, first_moment, second_moment, expert_ids, bucket_offsets, writer_rank):

time: 129 us -> 128 us (level)
  local copies, waits for them, and re-layouts: 2.45 us -> 0 us
  Pallas kernels: 125 us -> 127 us
    pallas_call x0 -> x1, Pallas kernels: none -> 2.56 us  [exchange(): pl.pallas_call(functools.partial(last_kernel, split), out_shape=jax.Shape...]
    unnamed x1 -> x0, local copies, waits for them, and re-layouts: 2.45 us -> none
where the time goes in v4:
time: 128 us; the launch traced here: 127 us
  Pallas kernels  127 us (99%)
    pallas_call x1, Pallas kernels, exchange(): pl.pallas_call(functools.partial(exchange_kernel, n_ep, n_dp, split), out...  125 us

profile of v4, /device:TPU:1, one launch (start us, length us, event | category | flops | bytes accessed | tf_op | source)
XLA Modules:
  0.0 127.4 jit_solution(6396397596735746060)
XLA Ops:
  0.0 124.9 %shard_map.64 = (bf16[3,8,32,3584]{3,2,1,0:T(8,128)(2,1)S(1)}, bf16[8,32,1024]{2,1,0:T(8,128)(2,1)S(1)}, bf16[256,256]{1,0:T(8,128)(2,1)S(1)}) custom-call(s32[8]{0:T(128)} %refs_in_0_.1, s32[1,1024]{1,0:T(1,128)} %bitcast.11, s32[1,1024]{1,0:T(1,128)} %bitcast.12, f32[256,3584]{1,0:T(8,128)} %bitcast.8, f32[256,3584]{1,0:T(8,128)} %bitcast.9, ...), custom_call_target="tpu_custom_call" | custom-call | tf_op jit(solution)/shard_map/pallas_call | solution.py:437
  124.9 2.6 %shard_map.65 = bf16[3,8,32,3584]{3,2,1,0:T(8,128)(2,1)} custom-call(bf16[3,8,32,3584]{3,2,1,0:T(8,128)(2,1)S(1)} %get-tuple-element.8.most_ref, bf16[8,32,1024]{2,1,0:T(8,128)(2,1)S(1)} %get-tuple-element.9.late_ref, bf16[256,256]{1,0:T(8,128)(2,1)S(1)} %get-tuple-element.10.after_ref), custom_call_target="tpu_custom_call" | custom-call | tf_op jit(solution)/shard_map/pallas_call | solution.py:479

commit v5 on v4

--- a/solution.py
+++ b/solution.py
@@ -91,7 +91,7 @@
 
 def last_kernel(split, most_ref, late_ref, after_ref, out_ref, placed, store):
     blocks, depth, cols = most_ref.shape[1:]
-    parts = 4 if blocks % 4 == 0 else 1
+    parts = 1
     some = blocks // parts
     f = FIELDS - 1
 
@@ -131,7 +131,7 @@
     placed, early, late = take(FIELDS), take(FIELDS), take(FIELDS - 1) + [last_late]
     ids_ref, offsets_ref, writers_ref = take(3)
     rank_ref, order_ref, position_ref, target_ref, arrives_ref, before, ahead = take(7)
-    load, z_send, z_recv, a_send, a_recv, b_send, b_recv, index_load = scratch
+    load, leave, z_recv, a_recv, b_recv, index_load = scratch
     ep, dp = lax.axis_index("ep"), lax.axis_index("dp")
     _, blocks, depth, cols = out_ref.shape
     rows = blocks * depth
@@ -188,7 +188,7 @@
         return [
             remote(
                 src.at[pl.ds(partner(dp, o, n_dp) * m_dp, m_dp)], dst.at[pl.ds(dp * m_dp, m_dp)],
-                z_send.at[c], z_recv.at[c], "dp", partner(dp, o, n_dp),
+                leave.at[0], z_recv.at[c], "dp", partner(dp, o, n_dp),
             )
             for o in z_order
         ]
@@ -197,7 +197,7 @@
         return [
             remote(
                 a_ref(c).at[pl.ds(partner(ep, o, n_ep) * m_ep, m_ep)], e1[c].at[ep],
-                a_send.at[c], a_recv.at[c], "ep", partner(ep, o, n_ep),
+                leave.at[1], a_recv.at[c], "ep", partner(ep, o, n_ep),
             )
             for o in e_order
         ]
@@ -206,7 +206,7 @@
         return [
             remote(
                 sel[c].at[partner(ep, o, n_ep)], b_ref(c).at[pl.ds(ep * m_ep, m_ep)],
-                b_send.at[c], b_recv.at[c], "ep", partner(ep, o, n_ep),
+                leave.at[2], b_recv.at[c], "ep", partner(ep, o, n_ep),
             )
             for o in e_order
         ]
@@ -214,18 +214,18 @@
     def z_all(c):
         src, dst = z_refs(c)
         part = pl.ds(0, (n_dp - 1) * m_dp)
-        return remote(src.at[part], dst.at[part], z_send.at[c], z_recv.at[c], "dp", partner(dp, 1, n_dp))
+        return remote(src.at[part], dst.at[part], leave.at[0], z_recv.at[c], "dp", partner(dp, 1, n_dp))
 
     def a_all(c):
         part = pl.ds(0, (n_ep - 1) * m_ep)
         return remote(
-            a_ref(c).at[part], e1[c].at[pl.ds(0, n_ep - 1)], a_send.at[c], a_recv.at[c], "ep", partner(ep, 1, n_ep)
+            a_ref(c).at[part], e1[c].at[pl.ds(0, n_ep - 1)], leave.at[1], a_recv.at[c], "ep", partner(ep, 1, n_ep)
         )
 
     def b_all(c):
         part = pl.ds(0, (n_ep - 1) * m_ep)
         return remote(
-            sel[c].at[pl.ds(0, n_ep - 1)], b_ref(c).at[part], b_send.at[c], b_recv.at[c], "ep", partner(ep, 1, n_ep)
+            sel[c].at[pl.ds(0, n_ep - 1)], b_ref(c).at[part], leave.at[2], b_recv.at[c], "ep", partner(ep, 1, n_ep)
         )
 
     def start(copies):
@@ -360,7 +360,6 @@
         z_all(c).wait_recv()
         permute(after, late[c - FIELDS], out_ref.at[c - FIELDS, :, :, span(c)])
 
-    narrow(5)
     for copy in index_copies:
         copy.wait()
     make_position()
@@ -368,8 +367,9 @@
         before[...] = one_hot(position_ref, 0, rows)
     sort(0)
     pl.semaphore_wait(barrier, n_dp + n_ep - 2)
+    z_start(0)
+    narrow(5)
     a_start(5)
-    z_start(0)
     narrow(3)
     a_start(3)
     sort(1)
@@ -411,10 +411,10 @@
     b_all(1).wait_recv()
     z_all(5).wait_recv()
     b_all(2).wait_recv()
-    for c in range(chunks):
-        z_all(c).wait_send()
-        a_all(c).wait_send()
-        b_all(c).wait_send()
+    for i, (axis, n, peers) in enumerate((("dp", n_dp, m_dp), ("ep", n_ep, m_ep), ("ep", n_ep, m_ep))):
+        part = out_ref.at[:, pl.ds(0, (n - 1) * peers)]
+        me = dp if axis == "dp" else ep
+        remote(part, part, leave.at[i], z_recv.at[0], axis, partner(me, 1, n)).wait_send()
 
 
 def exchange(expert_ids, offsets, writers, arrays, n_ep, n_dp):
@@ -463,9 +463,7 @@
             pltpu.VMEM(square, BF16),
             pltpu.VMEM((rows, rows), BF16),
             dma((chunks,)),
-            dma((chunks,)),
-            dma((chunks,)),
-            dma((chunks,)),
+            dma((3,)),
             dma((chunks,)),
             dma((chunks,)),
             dma((chunks,)),
@@ -481,7 +479,7 @@
         out_shape=jax.ShapeDtypeStruct((FIELDS, blocks, depth, cols), BF16),
         in_specs=[vmem] * 3,
         out_specs=pl.BlockSpec(memory_space=pl.ANY),
-        scratch_shapes=[pltpu.VMEM((blocks, depth, last[-1]), BF16), dma((FIELDS + 1, 4))],
+        scratch_shapes=[pltpu.VMEM((blocks, depth, last[-1]), BF16), dma((FIELDS + 1, 1))],
         compiler_params=pltpu.CompilerParams(vmem_limit_bytes=8 * 2**20),
     )(*in_vmem)
 

time: 128 us -> 127 us (level)
  no operation moved by 1% of the time
where the time goes in v5:
time: 127 us
  Pallas kernels  127 us (100%)
    pallas_call x1, Pallas kernels, exchange(): pl.pallas_call(functools.partial(exchange_kernel, n_ep, n_dp, split), out...  125 us

profile of v5, /device:TPU:1, one launch (start us, length us, event | category | flops | bytes accessed | tf_op | source)
XLA Modules:
  0.0 127.3 jit_solution(9158995139935697139)
XLA Ops:
  0.0 124.8 %shard_map.64 = (bf16[3,8,32,3584]{3,2,1,0:T(8,128)(2,1)S(1)}, bf16[8,32,1024]{2,1,0:T(8,128)(2,1)S(1)}, bf16[256,256]{1,0:T(8,128)(2,1)S(1)}) custom-call(s32[8]{0:T(128)} %refs_in_0_.1, s32[1,1024]{1,0:T(1,128)} %bitcast.11, s32[1,1024]{1,0:T(1,128)} %bitcast.12, f32[256,3584]{1,0:T(8,128)} %bitcast.8, f32[256,3584]{1,0:T(8,128)} %bitcast.9, ...), custom_call_target="tpu_custom_call" | custom-call | tf_op jit(solution)/shard_map/pallas_call | solution.py:437
  124.8 2.5 %shard_map.65 = bf16[3,8,32,3584]{3,2,1,0:T(8,128)(2,1)} custom-call(bf16[3,8,32,3584]{3,2,1,0:T(8,128)(2,1)S(1)} %get-tuple-element.8.most_ref, bf16[8,32,1024]{2,1,0:T(8,128)(2,1)S(1)} %get-tuple-element.9.late_ref, bf16[256,256]{1,0:T(8,128)(2,1)S(1)} %get-tuple-element.10.after_ref), custom_call_target="tpu_custom_call" | custom-call | tf_op jit(solution)/shard_map/pallas_call | solution.py:477
